TPU v7x, 32 devices: a whole 2x2x4 slice. The times are simulated.
32 devices in a mesh: row: 8 (over y, x, core), col: 4 (over z).
Axes of the slice: x: 2, y: 2, z: 4, core: 2. Of those that a mesh axis runs over, the one named last changes fastest.
Arguments:
- queries: bfloat16 [8, 128, 4096], P(None, 'row', 'col'), may hold values from -13 to 13, as said below
- key_cache: bfloat16 [8, 16384, 1024], P(None, ('row', 'col')), may hold values from -13 to 13
- value_cache: bfloat16 [8, 16384, 1024], P(None, ('row', 'col')), may hold values from -6 to 6
- key_table: bfloat16 [1024, 1024], replicated, may hold values from -24 to 24
- value_table: bfloat16 [1024, 1024], replicated, may hold values from -6 to 6
- lengths: int32 [8], replicated, may hold values from 2048 to 16384
- token_ids: int32 [8, 128], P(None, 'row'), may hold values from 0 to 1023
Outputs:
- attended: bfloat16 [8, 128, 4096], P(None, 'row', 'col')
Inputs may be any that keep to these rules, and one draw needn't show every extreme that they name: `queries`: entries of the query array lie in the stated range.
All inputs are finite; a program needn't handle non-finite values.
Results may differ from a plain program's by a relative error of at most 0.006.
Values may be sent and summed in bfloat16 or wider, within the bound.
A program may use at most 192 MiB of HBM per device.

v0:
```python
import jax
import jax.numpy as jnp
from jax import lax
from jax.sharding import PartitionSpec as P

HQ = 32
KH = 8
HD = 128


def cache_partials(whole, key_cache, value_cache, lengths, offset):
    users, beams, width = whole.shape
    positions = key_cache.shape[1]
    group = HQ // KH
    scale = HD ** (-0.5)

    def one_user(items):
        q_user, k_user, v_user, limit = items
        q_heads = q_user.reshape(beams, KH, group, HD)
        k_heads = k_user.reshape(positions, KH, HD)
        v_heads = v_user.reshape(positions, KH, HD)
        s = (
            jnp.einsum("wkgd,lkd->kwgl", q_heads, k_heads, preferred_element_type=jnp.float32)
            * scale
        )
        live = offset + jnp.arange(positions, dtype=jnp.int32) < limit
        s = jnp.where(live, s, -1e30)
        peak = jnp.max(s, axis=-1)
        weight = jnp.where(live, jnp.exp(s - peak[..., None]), 0.0)
        total = jnp.sum(weight, axis=-1)
        numer = jnp.einsum(
            "kwgl,lkd->wkgd",
            weight.astype(jnp.bfloat16),
            v_heads,
            preferred_element_type=jnp.float32,
        )
        peak = jnp.transpose(peak, (1, 0, 2)).reshape(beams, HQ)
        total = jnp.transpose(total, (1, 0, 2)).reshape(beams, HQ)
        return (numer.reshape(beams, width), peak, total)

    return lax.map(one_user, (whole, key_cache, value_cache, lengths))


def body(queries, key_cache, value_cache, key_table, value_table, lengths, token_ids):
    users, beam_part, width_part = queries.shape
    heads_part = width_part // HD
    scale = HD ** (-0.5)
    row_at = lax.axis_index("row")
    col_at = lax.axis_index("col")
    whole = lax.all_gather(queries, "col", axis=2, tiled=True)
    whole = lax.all_gather(whole, "row", axis=1, tiled=True)
    offset = (row_at * lax.axis_size("col") + col_at) * key_cache.shape[1]
    numer_part, peak_part, total_part = cache_partials(
        whole, key_cache, value_cache, lengths, offset
    )
    peak_all = lax.pmax(peak_part, ("row", "col"))
    factor = jnp.exp(peak_part - peak_all)
    weighted = (numer_part.reshape(users, -1, HQ, HD) * factor[..., None]).reshape(
        users, -1, HQ * HD
    )
    mass = total_part * factor

    def local_part(array, per_head):
        picked = lax.dynamic_slice_in_dim(array, row_at * beam_part, beam_part, 1)
        return lax.dynamic_slice_in_dim(
            picked, col_at * heads_part * per_head, heads_part * per_head, 2
        )

    numer, total = lax.psum((weighted, mass), ("row", "col"))
    numer = local_part(numer, HD)
    total = local_part(total, 1)
    peak = local_part(peak_all, 1)
    codes = jnp.arange(key_table.shape[0], dtype=jnp.int32)
    onehot = (token_ids[..., None] == codes).astype(jnp.bfloat16)
    own_keys = jnp.einsum("uwv,vc->uwc", onehot, key_table, preferred_element_type=jnp.float32)
    own_values = jnp.einsum("uwv,vc->uwc", onehot, value_table, preferred_element_type=jnp.float32)
    group = HQ // KH
    own_keys = jnp.repeat(own_keys.reshape(users, beam_part, KH, HD), group, axis=2)
    own_values = jnp.repeat(own_values.reshape(users, beam_part, KH, HD), group, axis=2)
    own_keys = lax.dynamic_slice_in_dim(own_keys, col_at * heads_part, heads_part, 2)
    own_values = lax.dynamic_slice_in_dim(own_values, col_at * heads_part, heads_part, 2)
    q_local = queries.astype(jnp.float32).reshape(users, beam_part, heads_part, HD)
    own_score = jnp.sum(q_local * own_keys, axis=-1) * scale
    final_peak = jnp.maximum(peak, own_score)
    carried = jnp.exp(peak - final_peak)
    fresh = jnp.exp(own_score - final_peak)
    numer = (
        numer.reshape(users, beam_part, heads_part, HD) * carried[..., None]
        + fresh[..., None] * own_values
    )
    total = total * carried + fresh
    result = numer / total[..., None]
    return result.reshape(users, beam_part, width_part).astype(jnp.bfloat16)


def solution(mesh):
    return jax.shard_map(
        body,
        mesh=mesh,
        in_specs=(
            P(None, "row", "col"),
            P(None, ("row", "col"), None),
            P(None, ("row", "col"), None),
            P(),
            P(),
            P(),
            P(None, "row"),
        ),
        out_specs=P(None, "row", "col"),
        check_vma=False,
    )
```

profile of v0, /device:TPU:0, one launch (start us, length us, event | category | flops | bytes accessed | tf_op | source)
XLA Modules:
  0.0 730.9 jit_solution(4568035272929321944)
XLA Ops:
  6.5 1.9 copy.35
  8.6 31.1 %all-gather.3.cloned.1.call-done = bf16[8,16,4096]{2,0,1:T(8,128)(2,1)} async-done(((bf16[8,16,1024]{2,0,1:T(8,128)(2,1)}), bf16[8,16,4096]{2,0,1:T(8,128)(2,1)}) %all-gather.3.cloned.1.call-update) | async-done | bytes 1048592 | tf_op jit(solution)/shard_map/all_gather | solution.py:50
  39.8 55.4 %all-gather.5.cloned.1.call-done = bf16[8,128,4096]{2,0,1:T(8,128)(2,1)} async-done(((bf16[8,16,4096]{2,0,1:T(8,128)(2,1)}), bf16[8,128,4096]{2,0,1:T(8,128)(2,1)}) %all-gather.5.cloned.1.call-update) | async-done | bytes 8388624 | tf_op jit(solution)/shard_map/all_gather | solution.py:51
  95.2 12.5 %copy.37 = bf16[8,128,4096]{1,2,0:T(8,128)(2,1)} copy(bf16[8,128,4096]{2,0,1:T(8,128)(2,1)} %all-gather.5.cloned.1.call-done) | data formatting | bytes 16777216 | tf_op jit(solution)/shard_map/while | solution.py:41
  107.7 186.9 %while.14 = (s32[]{:T(128)}, f32[8,128,4096]{1,2,0:T(8,128)}, f32[8,128,32]{1,2,0:T(8,128)}, f32[8,128,32]{1,2,0:T(8,128)S(1)}, bf16[8,512,1024]{2,1,0:T(8,128)(...) while((s32[]{:T(128)}, f32[8,128,4096]{1,2,0:T(8,128)}, ...), condition=%wide.region_3.4_spmd, body=%wide.region_0.3_spmd.sunk | while | flops 1100997632 | bytes 78777504 | solution.py:41
  110.3 1.4 copy.58
  112.9 2.8 fusion.35
  115.8 3.2 copy-done.1
  119.0 2.3 fusion.37
  123.3 1.4 copy.57
  124.6 5.0 fusion.36
  129.6 1.5 constant_dynamic-update-slice_fusion.2
  133.6 1.4 copy.58
  136.3 2.8 fusion.35
  139.1 3.2 copy-done.1
  142.4 2.3 fusion.37
  146.6 1.4 copy.57
  148.0 5.0 fusion.36
  152.9 1.5 constant_dynamic-update-slice_fusion.2
  157.0 1.4 copy.58
  159.6 2.8 fusion.35
  162.5 3.2 copy-done.1
  165.7 2.3 fusion.37
  170.0 1.4 copy.57
  171.3 5.0 fusion.36
  176.3 1.5 constant_dynamic-update-slice_fusion.2
  180.3 1.4 copy.58
  183.0 2.8 fusion.35
  185.8 3.2 copy-done.1
  189.1 2.3 fusion.37
  193.3 1.4 copy.57
  194.7 5.0 fusion.36
  199.6 1.5 constant_dynamic-update-slice_fusion.2
  203.7 1.4 copy.58
  206.4 2.8 fusion.35
  209.2 3.2 copy-done.1
  212.4 2.3 fusion.37
  218.1 5.0 fusion.36
  223.0 1.5 constant_dynamic-update-slice_fusion.2
  227.1 1.4 copy.58
  229.7 2.8 fusion.35
  232.6 3.2 copy-done.1
  235.8 2.3 fusion.37
  241.4 5.0 fusion.36
  246.4 1.5 constant_dynamic-update-slice_fusion.2
  250.5 1.4 copy.58
  253.1 2.8 fusion.35
  256.0 3.2 copy-done.1
  259.2 2.3 fusion.37
  264.8 5.0 fusion.36
  269.8 1.5 constant_dynamic-update-slice_fusion.2
  273.8 1.4 copy.58
  276.5 2.8 fusion.35
  279.3 3.2 copy-done.1
  282.6 2.3 fusion.37
  288.2 5.0 fusion.36
  293.1 1.4 constant_dynamic-update-slice_fusion.2
  294.7 124.8 %all-reduce.4.cloned.1.call-done = f32[8,128,32]{1,2,0:T(8,128)} async-done(((f32[8,128,32]{1,2,0:T(8,128)}), f32[8,128,32]{1,2,0:T(8,128)}) %all-reduce.4.cloned.1.call-update) | async-done | bytes 131088 | tf_op jit(solution)/shard_map/pmax | solution.py:56
  419.4 1.7 fusion.20
  421.1 11.3 %bitcast_multiply_fusion = f32[8,128,4096]{1,2,0:T(8,128)} fusion(f32[8,128,4096]{1,2,0:T(8,128)} %get-tuple-element.54, f32[8,128,32]{1,2,0:T(8,128)S(1)} %get-tuple-element.117), kind=kLoop, calls=%fused_computation.17 | loop fusion | flops 4194304 | bytes 33685504 | tf_op jit(solution)/shard_map/mul | solution.py:58
  434.6 2.1 fusion.9
  436.8 276.3 %all-reduce.6.cloned.1.call-done = (f32[8,128,4096]{1,2,0:T(8,128)}, f32[8,128,32]{1,2,0:T(8,128)}) async-done(((f32[8,128,4096]{1,2,0:T(8,128)}, f32[8,128,32]{1,2,0:T(8,128)}), (f32[8,128,4096]{1,2,0:T(8,128)}, f32[8,128,32]{1,2,0:T(8,128)})) %all-reduce.6.cloned.1.call-update) | async-done | bytes 16908304 | tf_op jit(solution)/shard_map/psum | solution.py:69
  714.4 5.3 constant_dynamic-slice_fusion.3
  719.7 2.8 copy.49
  (93 shorter events, 57.1 us)
Async XLA Ops:
  6.5 425.9 %copy-start = (bf16[1024,1024]{1,0:T(8,128)(2,1)S(1)}, bf16[1024,1024]{1,0:T(8,128)(2,1)}, u32[]{:S(2)}) copy-start(bf16[1024,1024]{1,0:T(8,128)(2,1)} %param.12) | copy-start | bytes 6291460
  6.5 33.1 %all-gather.3.cloned.1.call-start = ((), (), s32[]{:S(2)}) async-start(), calls=%async_computation | async-start | bytes 1310720 | tf_op jit(solution)/shard_map/all_gather | solution.py:50
  8.5 86.7 %all-gather.5.cloned.1.call-start = ((), (), s32[]{:S(2)}) async-start(), calls=%async_computation.1 | async-start | bytes 9437184 | tf_op jit(solution)/shard_map/all_gather | solution.py:51
  39.7 379.7 %all-reduce.4.cloned.1.call-start = ((), (), s32[]{:S(2)}) async-start(), calls=%async_computation.2 | async-start | bytes 262144 | tf_op jit(solution)/shard_map/pmax | solution.py:56
  39.8 67.9 %copy-start.4 = (s32[8]{0:T(128)S(1)}, s32[8]{0:T(128)}, u32[]{:S(2)}) copy-start(s32[8]{0:T(128)} %param.14) | copy-start | bytes 100
  115.8 3.2 copy-start.1
  139.1 3.2 copy-start.1
  162.5 3.2 copy-start.1
  185.8 3.2 copy-start.1
  209.2 3.2 copy-start.1
  232.6 3.2 copy-start.1
  256.0 3.2 copy-start.1
  279.3 3.2 copy-start.1
  294.6 418.6 %all-reduce.6.cloned.1.call-start = ((), (), s32[]{:S(2)}) async-start(), calls=%async_computation.3 | async-start | bytes 33816576 | tf_op jit(solution)/shard_map/psum | solution.py:69
  432.4 0.7 copy-start.3
  432.4 1.3 copy-start.2
Sparse Core Ops, SparseCore 0:
  8.9 30.6 all-gather.2
  41.5 53.6 all-gather.4
  294.7 124.6 all-reduce.3
  432.5 280.6 all-reduce.5
where the time goes:
time: 733 us; the launch traced here: 731 us
  waiting for transfers between devices  488 us (67%)
  local copies, waits for them, and re-layouts  126 us (17%)
  matrix products  65 us (9%)
  other arithmetic  38.3 us (5%)
  between operations  13.3 us (2%)
    psum x1, waiting for transfers between devices, body(): numer, total = lax.psum((weighted, mass), ('row', 'col'))  276 us
    pmax x1, waiting for transfers between devices, body(): peak_all = lax.pmax(peak_part, ('row', 'col'))  125 us
    dynamic_slice x48, local copies, waits for them, and re-layouts, cache_partials(): return lax.map(one_user, (whole, key_cache, value_cache, lengths))  57.9 us
    all_gather x1, waiting for transfers between devices, body(): whole = lax.all_gather(whole, 'row', axis=1, tiled=True)  55.4 us
    dot_general x8, matrix products, one_user(): jnp.einsum('kwgl,lkd->wkgd', weight.astype(jnp.bfloat16), v_heads, prefer...  39.7 us
    all_gather x1, waiting for transfers between devices, body(): whole = lax.all_gather(queries, 'col', axis=2, tiled=True)  31.1 us
    while x16, local copies, waits for them, and re-layouts  25.8 us
    dot_general x8, matrix products, one_user(): jnp.einsum('wkgd,lkd->kwgl', q_heads, k_heads, preferred_element_type=jnp...  22.7 us
  transfers between devices with their start and end apart: 4, of which 4 were waited for; matrix products, arithmetic and copies ran while one was open for 1% of the time, Pallas kernels for 0%

commit v1 on v0

--- a/solution.py
+++ b/solution.py
@@ -6,6 +6,17 @@
 HQ = 32
 KH = 8
 HD = 128
+
+
+def turned_line(x, mesh_axis, d):
+    size = lax.axis_size(mesh_axis)
+    right = [(i, (i + 1) % size) for i in range(size)]
+    blocks = [x]
+    for far in range(1, size):
+        blocks = [lax.ppermute(blocks[0], mesh_axis, right), *blocks]
+    whole = jnp.concatenate(blocks, axis=d)
+    turn = (lax.axis_index(mesh_axis) + 1) * blocks[-1].shape[d]
+    return jnp.roll(whole, turn, axis=d)
 
 
 def cache_partials(whole, key_cache, value_cache, lengths, offset):
@@ -48,7 +59,7 @@
     row_at = lax.axis_index("row")
     col_at = lax.axis_index("col")
     whole = lax.all_gather(queries, "col", axis=2, tiled=True)
-    whole = lax.all_gather(whole, "row", axis=1, tiled=True)
+    whole = turned_line(whole, "row", 1)
     offset = (row_at * lax.axis_size("col") + col_at) * key_cache.shape[1]
     numer_part, peak_part, total_part = cache_partials(
         whole, key_cache, value_cache, lengths, offset

time: 733 us -> 824 us (1.12)
  waiting for transfers between devices: 488 us -> 539 us
  local copies, waits for them, and re-layouts: 126 us -> 164 us
    ppermute x0 -> x7, waiting for transfers between devices: none -> 106 us  [turned_line(): blocks = [lax.ppermute(blocks[0], mesh_axis, right), *blocks]]
    all_gather x1 -> x0, waiting for transfers between devices: 55.4 us -> none  [body(): whole = lax.all_gather(whole, 'row', axis=1, tiled=True)]
    unnamed x12 -> x48, local copies, waits for them, and re-layouts: 2.84 us -> 33.8 us
    while x17 -> x16, local copies, waits for them, and re-layouts: 38.3 us -> 25.9 us
    dynamic_slice x48 -> x56, local copies, waits for them, and re-layouts: 57.9 us -> 68.1 us  [cache_partials(): return lax.map(one_user, (whole, key_cache, value_cache, lengths))]
  transfers between devices with their start and end apart: 4 -> 10, of which waited for: 4 -> 10; matrix products, arithmetic and copies ran while one was open for 1% -> 0% of each run, Pallas kernels for 0% -> 0%
where the time goes in v1:
time: 824 us; the launch traced here: 822 us
  waiting for transfers between devices  539 us (65%)
  local copies, waits for them, and re-layouts  164 us (20%)
  matrix products  67.5 us (8%)
  other arithmetic  38.4 us (5%)
  between operations  13.3 us (2%)
    psum x1, waiting for transfers between devices, body(): numer, total = lax.psum((weighted, mass), ('row', 'col'))  276 us
    pmax x1, waiting for transfers between devices, body(): peak_all = lax.pmax(peak_part, ('row', 'col'))  123 us
    ppermute x7, waiting for transfers between devices, turned_line(): blocks = [lax.ppermute(blocks[0], mesh_axis, right), *blocks]  106 us
    dynamic_slice x56, local copies, waits for them, and re-layouts, cache_partials(): return lax.map(one_user, (whole, key_cache, value_cache, lengths))  68.1 us
    dot_general x8, matrix products, one_user(): jnp.einsum('kwgl,lkd->wkgd', weight.astype(jnp.bfloat16), v_heads, prefer...  39.7 us
    unnamed x48, local copies, waits for them, and re-layouts  33.8 us
    all_gather x1, waiting for transfers between devices, body(): whole = lax.all_gather(queries, 'col', axis=2, tiled=True)  32.3 us
    while x16, local copies, waits for them, and re-layouts  25.9 us
  transfers between devices with their start and end apart: 10, of which 10 were waited for; matrix products, arithmetic and copies ran while one was open for 0% of the time, Pallas kernels for 0%

profile of v1, /device:TPU:0, one launch (start us, length us, event | category | flops | bytes accessed | tf_op | source)
XLA Modules:
  0.0 822.4 jit_solution(13502564973178384810)
XLA Ops:
  7.3 32.3 %all-gather.2.cloned.1.call-done = bf16[8,16,4096]{2,1,0:T(8,128)(2,1)} async-done(((bf16[8,16,1024]{2,1,0:T(8,128)(2,1)}), bf16[8,16,4096]{2,1,0:T(8,128)(2,1)}) %all-gather.2.cloned.1.call-update) | async-done | bytes 1048592 | tf_op jit(solution)/shard_map/all_gather | solution.py:61
  39.6 15.3 %collective-permute-done = bf16[8,16,4096]{2,1,0:T(8,128)(2,1)S(1)} collective-permute-done((bf16[8,16,4096]{2,1,0:T(8,128)(2,1)}, bf16[8,16,4096]{2,1,0:T(8,128)(2,1)S(1)}, u32[]{:S(2)}, u32[]{:S(2)}) %collective-permute-start) | collective-permute-done | bytes 1048608 | tf_op jit(solution)/shard_map/ppermute | solution.py:16
  56.0 15.1 %collective-permute-done.1 = bf16[8,16,4096]{2,1,0:T(8,128)(2,1)S(1)} collective-permute-done((bf16[8,16,4096]{2,1,0:T(8,128)(2,1)S(1)}, bf16[8,16,4096]{2,1,0:T(8,128)(2,1)S(1)}, u32[]{:S(2)}, u32[]{:S(2)}) %collective-permute-start.1) | collective-permute-done | bytes 1048608 | tf_op jit(solution)/shard_map/ppermute | solution.py:16
  72.1 15.1 %collective-permute-done.2 = bf16[8,16,4096]{2,1,0:T(8,128)(2,1)S(1)} collective-permute-done((bf16[8,16,4096]{2,1,0:T(8,128)(2,1)S(1)}, bf16[8,16,4096]{2,1,0:T(8,128)(2,1)S(1)}, u32[]{:S(2)}, u32[]{:S(2)}) %collective-permute-start.2) | collective-permute-done | bytes 1048608 | tf_op jit(solution)/shard_map/ppermute | solution.py:16
  88.2 15.1 %collective-permute-done.3 = bf16[8,16,4096]{2,1,0:T(8,128)(2,1)S(1)} collective-permute-done((bf16[8,16,4096]{2,1,0:T(8,128)(2,1)S(1)}, bf16[8,16,4096]{2,1,0:T(8,128)(2,1)S(1)}, u32[]{:S(2)}, u32[]{:S(2)}) %collective-permute-start.3) | collective-permute-done | bytes 1048608 | tf_op jit(solution)/shard_map/ppermute | solution.py:16
  104.3 15.1 %collective-permute-done.4 = bf16[8,16,4096]{2,1,0:T(8,128)(2,1)S(1)} collective-permute-done((bf16[8,16,4096]{2,1,0:T(8,128)(2,1)S(1)}, bf16[8,16,4096]{2,1,0:T(8,128)(2,1)S(1)}, u32[]{:S(2)}, u32[]{:S(2)}) %collective-permute-start.4) | collective-permute-done | bytes 1048608 | tf_op jit(solution)/shard_map/ppermute | solution.py:16
  120.4 15.2 %collective-permute-done.5 = bf16[8,16,4096]{2,1,0:T(8,128)(2,1)} collective-permute-done((bf16[8,16,4096]{2,1,0:T(8,128)(2,1)S(1)}, bf16[8,16,4096]{2,1,0:T(8,128)(2,1)}, u32[]{:S(2)}, u32[]{:S(2)}) %collective-permute-start.5) | collective-permute-done | bytes 1048608 | tf_op jit(solution)/shard_map/ppermute | solution.py:16
  135.7 15.4 %collective-permute-done.6 = bf16[8,16,4096]{2,1,0:T(8,128)(2,1)} collective-permute-done((bf16[8,16,4096]{2,1,0:T(8,128)(2,1)}, bf16[8,16,4096]{2,1,0:T(8,128)(2,1)}, u32[]{:S(2)}, u32[]{:S(2)}) %collective-permute-start.6) | collective-permute-done | bytes 1048608 | tf_op jit(solution)/shard_map/ppermute | solution.py:16
  151.1 2.3 constant_dynamic-update-slice_fusion.16
  153.3 2.3 constant_dynamic-update-slice_fusion.15
  155.6 2.3 constant_dynamic-update-slice_fusion.14
  157.9 2.3 constant_dynamic-update-slice_fusion.13
  160.2 2.3 constant_dynamic-update-slice_fusion.12
  162.4 2.3 constant_dynamic-update-slice_fusion.11
  164.7 2.3 constant_dynamic-update-slice_fusion.10
  167.0 2.3 constant_dynamic-update-slice_fusion.9
  169.3 2.3 constant_dynamic-update-slice_fusion.8
  171.5 2.3 constant_dynamic-update-slice_fusion.7
  180.1 7.7 constant_dynamic-slice_fusion.4
  187.8 199.8 %while.14 = (s32[]{:T(128)}, f32[8,128,4096]{1,2,0:T(8,128)}, f32[8,128,32]{1,2,0:T(8,128)}, f32[8,128,32]{1,2,0:T(8,128)S(1)}, bf16[8,512,1024]{2,1,0:T(8,128)(...) while((s32[]{:T(128)}, f32[8,128,4096]{1,2,0:T(8,128)}, ...), condition=%wide.region_3.4_spmd, body=%wide.region_0.3_spmd.sunk | while | flops 1100997632 | bytes 80874656 | solution.py:52
  194.3 3.2 fusion.35
  197.5 3.2 copy-done.1
  200.7 2.3 fusion.37
  206.3 5.0 fusion.36
  211.3 1.5 constant_dynamic-update-slice_fusion.18
  219.3 3.2 fusion.35
  222.5 3.2 copy-done.1
  225.7 2.3 fusion.37
  231.3 5.0 fusion.36
  244.2 3.2 fusion.35
  247.4 3.2 copy-done.1
  250.7 2.3 fusion.37
  256.3 5.0 fusion.36
  261.2 1.5 constant_dynamic-update-slice_fusion.18
  269.2 3.2 fusion.35
  272.4 3.2 copy-done.1
  275.6 2.3 fusion.37
  281.2 5.0 fusion.36
  286.2 1.5 constant_dynamic-update-slice_fusion.18
  294.2 3.2 fusion.35
  297.4 3.2 copy-done.1
  300.6 2.3 fusion.37
  306.3 5.0 fusion.36
  311.2 1.5 constant_dynamic-update-slice_fusion.18
  319.3 3.2 fusion.35
  322.4 3.2 copy-done.1
  325.7 2.3 fusion.37
  331.3 5.0 fusion.36
  336.3 1.5 constant_dynamic-update-slice_fusion.18
  344.2 3.2 fusion.35
  347.4 3.2 copy-done.1
  350.7 2.3 fusion.37
  356.3 5.0 fusion.36
  369.2 3.2 fusion.35
  372.4 3.2 copy-done.1
  375.6 2.3 fusion.37
  381.2 5.0 fusion.36
  387.9 123.0 %all-reduce.4.cloned.1.call-done = f32[8,128,32]{1,2,0:T(8,128)} async-done(((f32[8,128,32]{1,2,0:T(8,128)}), f32[8,128,32]{1,2,0:T(8,128)}) %all-reduce.4.cloned.1.call-update) | async-done | bytes 131088 | tf_op jit(solution)/shard_map/pmax | solution.py:67
  510.9 1.7 fusion.20
  512.5 11.3 %bitcast_multiply_fusion = f32[8,128,4096]{1,2,0:T(8,128)} fusion(f32[8,128,4096]{1,2,0:T(8,128)} %get-tuple-element.54, f32[8,128,32]{1,2,0:T(8,128)S(1)} %get-tuple-element.117), kind=kLoop, calls=%fused_computation.17 | loop fusion | flops 4194304 | bytes 33685504 | tf_op jit(solution)/shard_map/mul | solution.py:69
  526.1 2.1 fusion.9
  528.3 276.3 %all-reduce.6.cloned.1.call-done = (f32[8,128,4096]{1,2,0:T(8,128)}, f32[8,128,32]{1,2,0:T(8,128)}) async-done(((f32[8,128,4096]{1,2,0:T(8,128)}, f32[8,128,32]{1,2,0:T(8,128)}), (f32[8,128,4096]{1,2,0:T(8,128)}, f32[8,128,32]{1,2,0:T(8,128)})) %all-reduce.6.cloned.1.call-update) | async-done | bytes 16908304 | tf_op jit(solution)/shard_map/psum | solution.py:80
  805.8 5.3 constant_dynamic-slice_fusion.3
  811.1 2.8 copy.47
  (149 shorter events, 100.0 us)
Async XLA Ops:
  6.5 517.3 %copy-start = (bf16[1024,1024]{1,0:T(8,128)(2,1)S(1)}, bf16[1024,1024]{1,0:T(8,128)(2,1)}, u32[]{:S(2)}) copy-start(bf16[1024,1024]{1,0:T(8,128)(2,1)} %param.12) | copy-start | bytes 6291460
  6.5 33.1 %all-gather.2.cloned.1.call-start = ((), (), s32[]{:S(2)}) async-start(), calls=%async_computation | async-start | bytes 1310720 | tf_op jit(solution)/shard_map/all_gather | solution.py:61
  7.3 503.6 %all-reduce.4.cloned.1.call-start = ((), (), s32[]{:S(2)}) async-start(), calls=%async_computation.1 | async-start | bytes 262144 | tf_op jit(solution)/shard_map/pmax | solution.py:67
  39.6 139.4 %copy-start.2 = (bf16[8,16,4096]{2,1,0:T(8,128)(2,1)S(1)}, bf16[8,16,4096]{2,1,0:T(8,128)(2,1)}, u32[]{:S(2)}) copy-start(bf16[8,16,4096]{2,1,0:T(8,128)(2,1)} %all-gather.2.cloned.1.call-done) | copy-start | bytes 3145732
  39.6 15.3 %collective-permute-start = (bf16[8,16,4096]{2,1,0:T(8,128)(2,1)}, bf16[8,16,4096]{2,1,0:T(8,128)(2,1)S(1)}, u32[]{:S(2)}, u32[]{:S(2)}) collective-permute-start(bf16[8,16,4096]{2,1,0:T(8,128)(2,1)} %all-gather.2.cloned.1.call-done), channel_id=1, source_target_pairs={{0,4},{4,8},{8,12},{12,16},{16,20},{20,24},{24,28},{28,0},{1,5},{5... | collective-permute-start | bytes 3145736 | tf_op jit(solution)/shard_map/ppermute | solution.py:16
  55.0 1.0 copy-start.3
  56.0 15.1 %collective-permute-start.1 = (bf16[8,16,4096]{2,1,0:T(8,128)(2,1)S(1)}, bf16[8,16,4096]{2,1,0:T(8,128)(2,1)S(1)}, u32[]{:S(2)}, u32[]{:S(2)}) collective-permute-start(bf16[8,16,4096]{2,1,0:T(8,128)(2,1)S(1)} %collective-permute-done), channel_id=1, source_target_pairs={{0,4},{4,8},{8,12},{12,16},{16,20},{20,24},{24,28},{28,0},{1,5},{5... | collective-permute-start | bytes 3145736 | tf_op jit(solution)/shard_map/ppermute | solution.py:16
  71.1 1.0 copy-start.5
  72.1 15.1 %collective-permute-start.2 = (bf16[8,16,4096]{2,1,0:T(8,128)(2,1)S(1)}, bf16[8,16,4096]{2,1,0:T(8,128)(2,1)S(1)}, u32[]{:S(2)}, u32[]{:S(2)}) collective-permute-start(bf16[8,16,4096]{2,1,0:T(8,128)(2,1)S(1)} %collective-permute-done.1), channel_id=1, source_target_pairs={{0,4},{4,8},{8,12},{12,16},{16,20},{20,24},{24,28},{28,0},{1,5},{5... | collective-permute-start | bytes 3145736 | tf_op jit(solution)/shard_map/ppermute | solution.py:16
  87.2 1.0 copy-start.7
  88.2 15.1 %collective-permute-start.3 = (bf16[8,16,4096]{2,1,0:T(8,128)(2,1)S(1)}, bf16[8,16,4096]{2,1,0:T(8,128)(2,1)S(1)}, u32[]{:S(2)}, u32[]{:S(2)}) collective-permute-start(bf16[8,16,4096]{2,1,0:T(8,128)(2,1)S(1)} %collective-permute-done.2), channel_id=1, source_target_pairs={{0,4},{4,8},{8,12},{12,16},{16,20},{20,24},{24,28},{28,0},{1,5},{5... | collective-permute-start | bytes 3145736 | tf_op jit(solution)/shard_map/ppermute | solution.py:16
  103.3 1.0 copy-start.9
  104.3 15.1 %collective-permute-start.4 = (bf16[8,16,4096]{2,1,0:T(8,128)(2,1)S(1)}, bf16[8,16,4096]{2,1,0:T(8,128)(2,1)S(1)}, u32[]{:S(2)}, u32[]{:S(2)}) collective-permute-start(bf16[8,16,4096]{2,1,0:T(8,128)(2,1)S(1)} %collective-permute-done.3), channel_id=1, source_target_pairs={{0,4},{4,8},{8,12},{12,16},{16,20},{20,24},{24,28},{28,0},{1,5},{5... | collective-permute-start | bytes 3145736 | tf_op jit(solution)/shard_map/ppermute | solution.py:16
  119.5 1.0 copy-start.11
  120.4 15.2 %collective-permute-start.5 = (bf16[8,16,4096]{2,1,0:T(8,128)(2,1)S(1)}, bf16[8,16,4096]{2,1,0:T(8,128)(2,1)}, u32[]{:S(2)}, u32[]{:S(2)}) collective-permute-start(bf16[8,16,4096]{2,1,0:T(8,128)(2,1)S(1)} %collective-permute-done.4), channel_id=1, source_target_pairs={{0,4},{4,8},{8,12},{12,16},{16,20},{20,24},{24,28},{28,0},{1,5},{5... | collective-permute-start | bytes 3145736 | tf_op jit(solution)/shard_map/ppermute | solution.py:16
  135.6 15.4 %collective-permute-start.6 = (bf16[8,16,4096]{2,1,0:T(8,128)(2,1)}, bf16[8,16,4096]{2,1,0:T(8,128)(2,1)}, u32[]{:S(2)}, u32[]{:S(2)}) collective-permute-start(bf16[8,16,4096]{2,1,0:T(8,128)(2,1)} %collective-permute-done.5), channel_id=1, source_target_pairs={{0,4},{4,8},{8,12},{12,16},{16,20},{20,24},{24,28},{28,0},{1,5},{5... | collective-permute-start | bytes 3145736 | tf_op jit(solution)/shard_map/ppermute | solution.py:16
  135.6 38.2 %copy-start.12 = (bf16[8,16,4096]{2,1,0:T(8,128)(2,1)S(1)}, bf16[8,16,4096]{2,1,0:T(8,128)(2,1)}, u32[]{:S(2)}) copy-start(bf16[8,16,4096]{2,1,0:T(8,128)(2,1)} %copy-done.11) | copy-start | bytes 3145732
  135.7 39.2 %copy-start.10 = (bf16[8,16,4096]{2,1,0:T(8,128)(2,1)S(1)}, bf16[8,16,4096]{2,1,0:T(8,128)(2,1)}, u32[]{:S(2)}) copy-start(bf16[8,16,4096]{2,1,0:T(8,128)(2,1)} %copy-done.9) | copy-start | bytes 3145732
  135.7 40.2 %copy-start.8 = (bf16[8,16,4096]{2,1,0:T(8,128)(2,1)S(1)}, bf16[8,16,4096]{2,1,0:T(8,128)(2,1)}, u32[]{:S(2)}) copy-start(bf16[8,16,4096]{2,1,0:T(8,128)(2,1)} %copy-done.7) | copy-start | bytes 3145732
  135.7 41.2 %copy-start.6 = (bf16[8,16,4096]{2,1,0:T(8,128)(2,1)S(1)}, bf16[8,16,4096]{2,1,0:T(8,128)(2,1)}, u32[]{:S(2)}) copy-start(bf16[8,16,4096]{2,1,0:T(8,128)(2,1)} %copy-done.5) | copy-start | bytes 3145732
  135.7 42.3 %copy-start.4 = (bf16[8,16,4096]{2,1,0:T(8,128)(2,1)S(1)}, bf16[8,16,4096]{2,1,0:T(8,128)(2,1)}, u32[]{:S(2)}) copy-start(bf16[8,16,4096]{2,1,0:T(8,128)(2,1)} %copy-done.3) | copy-start | bytes 3145732
  169.3 18.6 %copy-start.15 = (s32[8]{0:T(128)S(1)}, s32[8]{0:T(128)}, u32[]{:S(2)}) copy-start(s32[8]{0:T(128)} %param.14) | copy-start | bytes 100
  197.5 3.3 copy-start.1
  222.5 3.3 copy-start.1
  247.4 3.3 copy-start.1
  272.4 3.3 copy-start.1
  297.4 3.3 copy-start.1
  322.4 3.3 copy-start.1
  347.4 3.3 copy-start.1
  372.4 3.3 copy-start.1
  387.7 416.9 %all-reduce.6.cloned.1.call-start = ((), (), s32[]{:S(2)}) async-start(), calls=%async_computation.2 | async-start | bytes 33816576 | tf_op jit(solution)/shard_map/psum | solution.py:80
  523.8 0.7 copy-start.14
  523.8 1.3 copy-start.13
Sparse Core Ops, SparseCore 0:
  8.9 30.6 all-gather.1
  387.8 123.0 all-reduce.3
  524.0 280.6 all-reduce.5
